TPU v7x, 64 devices: a 2x2x8 block of a 4x4x8 slice. The times are simulated.
64 devices in a mesh: dp: 4 (over x, y), sp: 16 (over z, core).
Axes of the slice: x: 2, y: 2, z: 8, core: 2. Of those that a mesh axis runs over, the one named last changes fastest.
The devices are a block of a 4x4x8 slice.
Arguments:
- q: bfloat16 [128, 64, 64], P('dp'), parts along dimension 0
- k: bfloat16 [128, 2048, 64, 64], P('dp', 'sp'), parts along dimension 0
- v: bfloat16 [128, 2048, 64, 64], P('dp', 'sp'), parts along dimension 0
Outputs:
- q: bfloat16 [128, 64, 64], P('dp'), parts along dimension 0
There are 4 independent parts. A program takes and returns all parts, laid end to end along the dimension named above; each array names one.
All inputs are finite; a program needn't handle non-finite values.
Results may differ from a plain program's by a relative error of at most 0.012.
Values are sent between devices in bfloat16 or wider.
A program may use at most 768 MiB of HBM per device.

v0:
```python
import jax
import jax.numpy as jnp
from jax import lax
from jax.sharding import PartitionSpec as P


def einsum(form, a, b):
    return jnp.einsum(form, a.astype(jnp.float32), b.astype(jnp.float32))


def part_of(q, k, v):
    grouped = q.reshape(q.shape[0], k.shape[2], -1, q.shape[2])
    scores = einsum("bgsd,bugd->bgsu", grouped, k) * q.shape[2] ** -0.5
    high = jnp.max(scores, -1, keepdims=True)
    weights = jnp.exp(scores - high)
    seen = einsum("bgsu,bugd->bgsd", weights.astype(jnp.bfloat16), v)
    return jnp.concatenate([seen, jnp.sum(weights, -1, keepdims=True), high], -1)


def together(parts):
    seen, total, high = parts[..., :-2], parts[..., -2:-1], parts[..., -1:]
    scale = jnp.exp(high - jnp.max(high, 0))
    return (jnp.sum(seen * scale, 0) / jnp.sum(total * scale, 0)).astype(jnp.bfloat16)


def solution(mesh):
    def step(q, k, v):
        return together(lax.all_gather(part_of(q, k, v), "sp")).reshape(q.shape)

    return jax.shard_map(
        step,
        mesh=mesh,
        in_specs=(P("dp", None, None), P("dp", "sp", None, None), P("dp", "sp", None, None)),
        out_specs=P("dp", None, None),
        check_vma=False,
    )
```

profile of v0, /device:TPU:21, one launch (start us, length us, event | category | flops | bytes accessed | tf_op | source)
XLA Modules:
  0.0 165.4 jit_solution(13509468822243421354)
XLA Ops:
  6.5 0.0 all-gather.3.cloned.1.call-start
  6.6 15.1 %fusion.3 = f32[32,64,1,128]{3,2,1,0:T(1,128)S(1)} fusion(bf16[32,128,64,64]{1,3,2,0:T(8,128)(2,1)} %param.4, bf16[32,64,64,1]{2,1,0,3:T(8,128)(2,1)} %bitcast.20), kind=kOutput, calls=%fused_computation.5 | convolution fusion | flops 33554432 | bytes 34865152 | tf_op jit(solution)/shard_map/bgsd,bugd->bgsu/dot_general | solution.py:8
  21.7 0.4 multiply_reduce_fusion
  22.1 0.7 fusion.7
  22.7 22.4 %fusion.1 = f32[32,64,1,64]{3,2,1,0:T(1,128)S(1)} fusion(bf16[32,128,64,64]{1,3,2,0:T(8,128)(2,1)} %param.5, bf16[32,64,128,1]{2,1,0,3:T(8,128)(2,1)S(1)} %get-tuple-element.7), kind=kOutput, calls=%fused_computation.3 | convolution fusion | flops 33554432 | bytes 34603008 | tf_op jit(solution)/shard_map/bgsu,bugd->bgsd/dot_general | solution.py:8
  45.1 0.8 copy.10
  45.9 1.1 pad_maximum_fusion
  47.0 0.1 all-gather.3.cloned.1.call-update
  47.1 99.6 %all-gather.3.cloned.1.call-done = f32[512,64,1,66]{1,0,3,2:T(8,128)} async-done(((f32[32,64,1,66]{1,0,3,2:T(8,128)}), f32[512,64,1,66]{1,0,3,2:T(8,128)}) %all-gather.3.cloned.1.call-update) | async-done | bytes 8650768 | tf_op jit(solution)/shard_map/all_gather | solution.py:28
  146.7 1.0 slice_reduce_fusion
  147.7 1.1 fusion.8
  148.8 8.2 %fusion = f32[32,64,64]{1,0,2:T(8,128)S(1)} fusion(f32[16,32,64,1,66]{2,1,0,4,3:T(8,128)} %bitcast.15, f32[16,32,64]{2,1,0:T(8,128)S(1)} %get-tuple-element.6), kind=kLoop, calls=%fused_computation.1 | loop fusion | flops 4063232 | bytes 9043968 | tf_op jit(solution)/shard_map/reduce_sum | solution.py:23
  157.0 0.1 divide_convert_fusion
  157.1 1.4 copy.6
Async XLA Ops:
  6.5 140.2 %all-gather.3.cloned.1.call-start = ((), (), s32[]{:S(2)}) async-start(), calls=%async_computation | async-start | bytes 18382848 | tf_op jit(solution)/shard_map/all_gather | solution.py:28
Sparse Core Ops, SparseCore 0:
  47.2 99.4 all-gather.2
where the time goes:
time: 166 us; the launch traced here: 165 us
  waiting for transfers between devices  99.7 us (60%)
  matrix products  37.5 us (23%)
  between operations  13.4 us (8%)
  other arithmetic  12.5 us (8%)
  local copies, waits for them, and re-layouts  2.16 us (1%)
    all_gather x1, waiting for transfers between devices, step(): return together(lax.all_gather(part_of(q, k, v), 'sp')).reshape(q.shape)  99.6 us
    dot_general x2, matrix products, einsum(): return jnp.einsum(form, a.astype(jnp.float32), b.astype(jnp.float32))  37.5 us
    reduce_sum x1, other arithmetic, together(): jnp.sum(seen * scale, 0) / jnp.sum(total * scale, 0)  8.2 us
  transfers between devices with their start and end apart: 1, of which 1 were waited for; matrix products, arithmetic and copies ran while one was open for 0% of the time, Pallas kernels for 0%

commit v1 on v0

v1 whole, which is shorter than its diff:
```python
import functools

import jax
import jax.numpy as jnp
from jax import lax
from jax.experimental import pallas as pl
from jax.experimental.pallas import tpu as pltpu
from jax.sharding import PartitionSpec as P

MESH = pl.DeviceIdType.MESH
F32, BF16 = jnp.float32, jnp.bfloat16
SLOTS = 6
ROWS = 16


def iota(shape, dim):
    return lax.broadcasted_iota(jnp.int32, shape, dim)


def scores_of(q, keys, head):
    heads = q.shape[0]
    per = 128 // head
    out = []
    for first in range(0, heads, ROWS):
        rows = q[first : first + ROWS]
        wide = jnp.concatenate([rows] * per, axis=1)
        blocks = [
            jnp.where(iota((ROWS, 128), 0) == iota((ROWS, 128), 1) // head + per * j, wide, jnp.zeros_like(wide))
            for j in range(ROWS // per)
        ]
        out.append(
            jnp.dot(
                jnp.concatenate(blocks, axis=1),
                keys[first * head : (first + ROWS) * head],
                preferred_element_type=F32,
            )
        )
    return jnp.concatenate(out, axis=0) * head**-0.5


def row_of(column, heads):
    own = iota((heads, 128), 1) % heads == iota((heads, 128), 0)
    return jnp.sum(jnp.where(own, column, 0.0), axis=0, keepdims=True)


def weights_of(scores):
    heads, tokens = scores.shape
    high = jnp.max(scores, axis=1, keepdims=True)
    weights = jnp.exp(scores - high)
    total = jnp.sum(weights, axis=1, keepdims=True)
    wide = lambda x: jnp.broadcast_to(x, (heads, 128))
    return weights.astype(BF16), row_of(wide(total), heads), row_of(wide(high), heads)


def seen_of(weights, values, head):
    heads, tokens = weights.shape
    half = heads // 2
    nothing = jnp.zeros((half, tokens), BF16)
    lower = jnp.concatenate([weights[:half], nothing] * (128 // heads), axis=0)
    upper = jnp.concatenate([nothing, weights[half:]] * (128 // heads), axis=0)
    both = jnp.concatenate([values[: half * head], values[half * head :]], axis=1)
    products = lax.dot_general(
        both, jnp.concatenate([lower, upper], axis=1), (((1,), (1,)), ((), ())), preferred_element_type=F32
    )
    lane = iota((head // 2, 128), 1)
    out = jnp.zeros((head // 2, 128), F32)
    for h in range(half):
        mine = products[h * head : (h + 1) * head]
        out = jnp.where(lane % half == h, jnp.where(lane < heads, mine[: head // 2], mine[head // 2 :]), out)
    return out


def kernel(
    n,
    q_ref,
    k_hbm,
    v_hbm,
    out_ref,
    kbuf,
    vbuf,
    part,
    stat,
    parts,
    stats,
    done,
    k_sem,
    v_sem,
    part_send,
    stat_send,
    part_recv,
    stat_recv,
    done_send,
    done_recv,
):
    me = lax.axis_index("sp")
    sequences = k_hbm.shape[0]
    heads = q_ref.shape[0] // sequences
    head = q_ref.shape[1]
    chips = n // 2
    chip, core = me // 2, me % 2

    def owner_of(t):
        j = t // 2
        away = (chips // 2 - (j + 1) // 2) * (2 * (j % 2) - 1)
        return (chip + away + chips) % chips * 2 + (core + 1 + t % 2) % 2

    def sequence_of(i):
        return i // n * n + owner_of(i % n)

    def k_copy(i):
        slot = i % SLOTS
        return pltpu.make_async_copy(k_hbm.at[sequence_of(i)], kbuf.at[slot], k_sem.at[slot])

    def v_copy(i):
        slot = i % SLOTS
        return pltpu.make_async_copy(v_hbm.at[sequence_of(i)], vbuf.at[slot], v_sem.at[slot])

    def part_copies(i):
        to = {"sp": owner_of(i % n)}
        return (
            pltpu.make_async_remote_copy(
                part.at[i], parts.at[i], part_send.at[i], part_recv.at[i], device_id=to, device_id_type=MESH
            ),
            pltpu.make_async_remote_copy(
                stat.at[i], stats.at[i], stat_send.at[i], stat_recv.at[i], device_id=to, device_id_type=MESH
            ),
        )

    def done_copy(r, t):
        mine = r * n + me
        return pltpu.make_async_remote_copy(
            done.at[mine],
            done.at[mine],
            done_send.at[r * n + t],
            done_recv.at[r * n + t],
            device_id={"sp": owner_of(t)},
            device_id_type=MESH,
        )

    def q_of(i):
        return q_ref[pl.ds(pl.multiple_of(sequence_of(i) * heads, heads), heads), :]

    def score(i):
        weights, total, high = weights_of(scores_of(q_of(i), kbuf.at[i % SLOTS], head))
        return weights, total, high

    def keep_stat(i, total, high):
        stat[i] = jnp.concatenate([total, high], axis=0)

    def see(i, weights):
        part[i] = seen_of(weights, vbuf.at[i % SLOTS], head).astype(BF16)

    def finish(r):
        own = r * n + n - 1
        for t in range(n - 1):
            for copy in part_copies(r * n + t):
                copy.wait_recv()
        parts[own] = part[own]
        stats[own] = stat[own]
        highs = [stats[r * n + t][1:2] for t in range(n)]
        high = functools.reduce(jnp.maximum, highs)
        total = jnp.zeros_like(high)
        seen = jnp.zeros(parts.shape[1:], F32)
        for t in range(n):
            scale = jnp.exp(highs[t] - high)
            total += stats[r * n + t][0:1] * scale
            seen += parts[r * n + t].astype(F32) * scale
        done[r * n + me] = (seen / total).astype(BF16)
        for t in range(n - 1):
            done_copy(r, t).start()

    for i in range(SLOTS):
        k_copy(i).start()
        if i < SLOTS - 1:
            v_copy(i).start()
    barrier = pltpu.get_barrier_semaphore()
    for away in range(1, n):
        pl.semaphore_signal(barrier, inc=1, device_id={"sp": (me + away) % n}, device_id_type=MESH)

    k_copy(0).wait()
    weights, total, high = score(0)
    keep_stat(0, total, high)
    pl.semaphore_wait(barrier, n - 1)

    def step(i, weights):
        k_copy(i + 1).wait()
        v_copy(i).wait()

        @pl.when(i + SLOTS < sequences)
        def _():
            k_copy(i + SLOTS).start()

        @pl.when(i + SLOTS - 1 < sequences)
        def _():
            v_copy(i + SLOTS - 1).start()

        @pl.when((i > 0) & (i % n != 0))
        def _():
            for copy in part_copies(i - 1):
                copy.start()

        later, total, high = score(i + 1)
        see(i, weights)
        keep_stat(i + 1, total, high)

        for r in range(sequences // n - 1):

            @pl.when(i == (r + 1) * n + n // 2)
            def _():
                finish(r)

        return later

    weights = lax.fori_loop(0, sequences - 1, step, weights)
    last = sequences - 1
    v_copy(last).wait()
    for copy in part_copies(last - 1):
        copy.start()
    see(last, weights)
    rounds = sequences // n
    finish(rounds - 1)
    for r in range(rounds):
        for t in range(n - 1):
            copy = done_copy(r, t)
            copy.wait_recv()
            copy.wait_send()
            for copy in part_copies(r * n + t):
                copy.wait_send()
    out_ref[...] = done[...]


def solution(mesh):
    n = mesh.shape["sp"]

    def step(q, k, v):
        sequences, tokens, heads, head = k.shape
        keys, values = (jnp.transpose(x, (0, 2, 3, 1)).reshape(sequences, heads * head, tokens) for x in (k, v))
        half = head // 2
        packed = (sequences, half, 2 * heads)
        out = pl.pallas_call(
            functools.partial(kernel, n),
            out_shape=jax.ShapeDtypeStruct(packed, BF16),
            in_specs=[
                pl.BlockSpec(memory_space=pltpu.VMEM),
                pl.BlockSpec(memory_space=pl.ANY),
                pl.BlockSpec(memory_space=pl.ANY),
            ],
            out_specs=pl.BlockSpec(memory_space=pltpu.VMEM),
            scratch_shapes=[
                pltpu.VMEM((SLOTS, heads * head, tokens), BF16),
                pltpu.VMEM((SLOTS, heads * head, tokens), BF16),
                pltpu.VMEM(packed, BF16),
                pltpu.VMEM((sequences, 2, 2 * heads), F32),
                pltpu.VMEM(packed, BF16),
                pltpu.VMEM((sequences, 2, 2 * heads), F32),
                pltpu.VMEM(packed, BF16),
                pltpu.SemaphoreType.DMA((SLOTS,)),
                pltpu.SemaphoreType.DMA((SLOTS,)),
                pltpu.SemaphoreType.DMA((sequences,)),
                pltpu.SemaphoreType.DMA((sequences,)),
                pltpu.SemaphoreType.DMA((sequences,)),
                pltpu.SemaphoreType.DMA((sequences,)),
                pltpu.SemaphoreType.DMA((sequences,)),
                pltpu.SemaphoreType.DMA((sequences,)),
            ],
            compiler_params=pltpu.CompilerParams(collective_id=0, has_side_effects=True),
        )(q.reshape(sequences * heads, head), keys, values)
        return out.reshape(sequences, half, 2, heads).transpose(0, 3, 2, 1).reshape(q.shape)

    return jax.shard_map(
        step,
        mesh=mesh,
        in_specs=(P("dp", None, None), P("dp", "sp", None, None), P("dp", "sp", None, None)),
        out_specs=P("dp", None, None),
        check_vma=False,
    )
```

time: 166 us -> 48.1 us (0.29)
  waiting for transfers between devices: 99.7 us -> 0 us
  Pallas kernels: 0 us -> 45.6 us
  matrix products: 37.5 us -> 0 us
  between operations: 13.4 us -> 0.02 us
  other arithmetic: 12.5 us -> 0 us
    all_gather x1 -> x0, waiting for transfers between devices: 99.6 us -> none  [step(): return together(lax.all_gather(part_of(q, k, v), 'sp')).reshape(q.shape)]
    pallas_call x0 -> x1, Pallas kernels: none -> 45.6 us  [step(): pl.pallas_call(functools.partial(kernel, n), out_shape=jax.ShapeDtypeStru...]
    dot_general x2 -> x0, matrix products: 37.5 us -> none  [einsum(): return jnp.einsum(form, a.astype(jnp.float32), b.astype(jnp.float32))]
    reduce_sum x2 -> x0, other arithmetic: 9.3 us -> none  [the longest x1 8.2 us: together(): jnp.sum(seen * scale, 0) / jnp.sum(total * scale, 0)]
    reshape x0 -> x3, local copies, waits for them, and re-layouts: none -> 2.31 us  [step(): out.reshape(sequences, half, 2, heads).transpose(0, 3, 2, 1)]
  transfers between devices with their start and end apart: 1 -> 0, of which waited for: 1 -> 0; matrix products, arithmetic and copies ran while one was open for 0% -> 0% of each run, Pallas kernels for 0% -> 0%
where the time goes in v1:
time: 48.1 us; the launch traced here: 48 us
  Pallas kernels  45.6 us (95%)
  local copies, waits for them, and re-layouts  2.31 us (5%)
    pallas_call x1, Pallas kernels, step(): pl.pallas_call(functools.partial(kernel, n), out_shape=jax.ShapeDtypeStru...  45.6 us
    reshape x3, local copies, waits for them, and re-layouts, step(): out.reshape(sequences, half, 2, heads).transpose(0, 3, 2, 1)  2.31 us

profile of v1, /device:TPU:21, one launch (start us, length us, event | category | flops | bytes accessed | tf_op | source)
XLA Modules:
  0.0 48.0 jit_solution(1689937594019711142)
XLA Ops:
  0.0 45.6 %shard_map.37 = bf16[32,32,128]{2,1,0:T(8,128)(2,1)} custom-call(bf16[2048,64]{1,0:T(8,128)(2,1)} %bitcast.13, bf16[32,4096,128]{2,1,0:T(8,128)(2,1)} %bitcast.10, bf16[32,4096,128]{2,1,0:T(8,128)(2,1)} %bitcast.11), custom_call_target="tpu_custom_call" | custom-call | tf_op jit(solution)/shard_map/pallas_call | solution.py:240
  45.7 1.2 %reshape.18 = bf16[32,32,2,64]{3,2,1,0:T(2,128)(2,1)S(1)} reshape(bf16[32,32,128]{2,1,0:T(8,128)(2,1)} %shard_map.37) | data formatting | bytes 524288 | tf_op jit(solution)/shard_map/reshape | solution.py:268
  46.9 0.1 copy.5
  47.0 1.0 %copy.6 = bf16[32,64,64]{2,1,0:T(8,128)(2,1)} copy(bf16[32,64,64]{1,2,0:T(8,128)(2,1)S(1)} %bitcast.12) | data formatting | bytes 524288 | tf_op jit(solution)/shard_map/reshape | solution.py:268

commit v2 on v1

v2 whole, which is shorter than its diff:
```python
import functools

import jax
import jax.numpy as jnp
from jax import lax
from jax.experimental import pallas as pl
from jax.experimental.pallas import tpu as pltpu
from jax.sharding import PartitionSpec as P

MESH = pl.DeviceIdType.MESH
F32, BF16 = jnp.float32, jnp.bfloat16
SLOTS = 4
EARLY = 3
ROWS = 16


def iota(shape, dim):
    return lax.broadcasted_iota(jnp.int32, shape, dim)


def scores_of(q, keys, head):
    heads = q.shape[0]
    per = 128 // head
    out = []
    for first in range(0, heads, ROWS):
        rows = q[first : first + ROWS]
        wide = jnp.concatenate([rows] * per, axis=1)
        blocks = [
            jnp.where(iota((ROWS, 128), 0) == iota((ROWS, 128), 1) // head + per * j, wide, jnp.zeros_like(wide))
            for j in range(ROWS // per)
        ]
        out.append(
            jnp.dot(
                jnp.concatenate(blocks, axis=1),
                keys[first * head : (first + ROWS) * head],
                preferred_element_type=F32,
            )
        )
    return jnp.concatenate(out, axis=0) * head**-0.5


def row_of(column, heads):
    own = iota((heads, 128), 1) % heads == iota((heads, 128), 0)
    return jnp.sum(jnp.where(own, column, 0.0), axis=0, keepdims=True)


def weights_of(scores):
    heads, tokens = scores.shape
    high = jnp.max(scores, axis=1, keepdims=True)
    weights = jnp.exp(scores - high)
    total = jnp.sum(weights, axis=1, keepdims=True)
    wide = lambda x: jnp.broadcast_to(x, (heads, 128))
    return weights.astype(BF16), row_of(wide(total), heads), row_of(wide(high), heads)


def seen_of(weights, values, head):
    heads, tokens = weights.shape
    half = heads // 2
    nothing = jnp.zeros((half, tokens), BF16)
    lower = jnp.concatenate([weights[:half], nothing] * (128 // heads), axis=0)
    upper = jnp.concatenate([nothing, weights[half:]] * (128 // heads), axis=0)
    both = jnp.concatenate([values[: half * head], values[half * head :]], axis=1)
    products = lax.dot_general(
        both, jnp.concatenate([lower, upper], axis=1), (((1,), (1,)), ((), ())), preferred_element_type=F32
    )
    lane = iota((head // 2, 128), 1)
    out = jnp.zeros((head // 2, 128), F32)
    for h in range(half):
        mine = products[h * head : (h + 1) * head]
        out = jnp.where(lane % half == h, jnp.where(lane < heads, mine[: head // 2], mine[head // 2 :]), out)
    return out


def turned(seen):
    rows = seen.T
    half, quarter = rows.shape[0] // 2, rows.shape[0] // 4
    return jnp.concatenate(
        [rows[:quarter], rows[half : half + quarter], rows[quarter:half], rows[half + quarter :]], axis=1
    )


def kernel(
    n,
    q_hbm,
    k_hbm,
    v_hbm,
    out_ref,
    q_ref,
    kbuf,
    vbuf,
    part,
    stat,
    parts,
    stats,
    done,
    q_sem,
    k_sem,
    v_sem,
    part_send,
    stat_send,
    part_recv,
    stat_recv,
    done_send,
    done_recv,
):
    me = lax.axis_index("sp")
    cores = 2
    chips = n // cores
    chip, core = lax.div(me, cores), lax.rem(me, cores)
    steps, rows = k_hbm.shape[0], k_hbm.shape[1]
    rounds = steps // chips
    heads = q_ref.shape[0] // (steps * cores)
    head = q_ref.shape[1]

    def chip_of(j):
        away = (chips // 2 - lax.div(j + 1, 2)) * (2 * lax.rem(j, 2) - 1)
        return lax.rem(chip + away + chips, chips)

    def block_of(i):
        return lax.div(i, chips) * chips + chip_of(lax.rem(i, chips))

    def k_copy(i):
        slot = lax.rem(i, SLOTS)
        return pltpu.make_async_copy(k_hbm.at[block_of(i)], kbuf.at[slot], k_sem.at[slot])

    def v_copy(i):
        slot = lax.rem(i, SLOTS)
        return pltpu.make_async_copy(v_hbm.at[block_of(i)], vbuf.at[slot], v_sem.at[slot])

    def send(i, other):
        r, j = lax.div(i, chips), lax.rem(i, chips)
        to = lax.rem(core + other, cores)
        slot = j * cores + 1 - other
        device = {"sp": chip_of(j) * cores + to}
        pltpu.make_async_remote_copy(
            part.at[i, to],
            parts.at[r, slot],
            part_send,
            part_recv.at[r],
            device_id=device,
            device_id_type=MESH,
        ).start()
        pltpu.make_async_remote_copy(
            stat.at[i, to],
            stats.at[r, slot],
            stat_send,
            stat_recv.at[r],
            device_id=device,
            device_id_type=MESH,
        ).start()

    def score(i, j):
        q = q_ref[pl.ds(pl.multiple_of((block_of(i) * cores + j) * heads, heads), heads), :]
        size = rows // cores
        keys = kbuf.at[lax.rem(i, SLOTS), j * size : (j + 1) * size]
        weights, total, high = weights_of(scores_of(q, keys, head))
        stat[i, j] = jnp.concatenate([total, high], axis=0)
        return weights

    def see(i, j, weights):
        size = rows // cores
        values = vbuf.at[lax.rem(i, SLOTS), j * size : (j + 1) * size]
        part[i, j] = seen_of(weights, values, head).astype(BF16)

    def wait_for(ref, sem):
        pltpu.make_async_copy(ref, ref, sem).wait()

    def finish(r):
        own = n - 1
        parts[r, own] = part[r * chips + chips - 1, core]
        stats[r, own] = stat[r * chips + chips - 1, core]
        wait_for(stats.at[r, : n - 1], stat_recv.at[r])
        highs = [stats[r, t][1:2] for t in range(n)]
        high = functools.reduce(jnp.maximum, highs)
        scales = [jnp.exp(x - high) for x in highs]
        total = functools.reduce(jnp.add, [stats[r, t][0:1] * scales[t] for t in range(n)])
        wait_for(parts.at[r, : n - 1], part_recv.at[r])
        seen = functools.reduce(jnp.add, [parts[r, t].astype(F32) * scales[t] for t in range(n)])
        done[r * n + me] = turned(seen / total).astype(BF16)
        for j in range(chips):
            for other in (1, 0):
                if j == chips - 1 and other == 0:
                    continue
                pltpu.make_async_remote_copy(
                    done.at[r * n + me],
                    done.at[r * n + me],
                    done_send,
                    done_recv.at[r],
                    device_id={"sp": chip_of(j) * cores + lax.rem(core + other, cores)},
                    device_id_type=MESH,
                ).start()

    q_copy = pltpu.make_async_copy(q_hbm, q_ref, q_sem)
    q_copy.start()
    for i in range(SLOTS):
        k_copy(i).start()
        if i < SLOTS - 1:
            v_copy(i).start()
    barrier = pltpu.get_barrier_semaphore()
    for away in range(1, n):
        pl.semaphore_signal(barrier, inc=1, device_id={"sp": lax.rem(me + away, n)}, device_id_type=MESH)

    q_copy.wait()
    k_copy(0).wait()
    weights = tuple(score(0, j) for j in range(cores))
    pl.semaphore_wait(barrier, n - 1)

    def step(i, weights):
        k_copy(i + 1).wait()
        v_copy(i).wait()

        @pl.when(i + SLOTS < steps)
        def _():
            k_copy(i + SLOTS).start()

        @pl.when(i + SLOTS - 1 < steps)
        def _():
            v_copy(i + SLOTS - 1).start()

        @pl.when(i > 0)
        def _():
            send(i - 1, 1)

        @pl.when(lax.rem(i, chips) > 0)
        def _():
            send(i - 1, 0)

        later = []
        for j in range(cores):
            later.append(score(i + 1, j))
            see(i, j, weights[j])
        return tuple(later)

    first = 0
    for r in range(rounds - 1):
        until = (r + 1) * chips + EARLY
        weights = lax.fori_loop(first, until, step, weights)
        finish(r)
        first = until
    weights = lax.fori_loop(first, steps - 1, step, weights)
    last = steps - 1
    v_copy(last).wait()
    send(last - 1, 1)
    send(last - 1, 0)
    for j in range(cores):
        see(last, j, weights[j])
    send(last, 1)
    finish(rounds - 1)
    wait_for(parts.at[:, : n - 1], part_send)
    wait_for(stats.at[:, : n - 1], stat_send)
    for r in range(rounds):
        wait_for(done.at[: n - 1], done_send)
    for r in range(rounds):
        wait_for(done.at[: n - 1], done_recv.at[r])
    out_ref[...] = done[...]


def solution(mesh):
    n = mesh.shape["sp"]

    def step(q, k, v):
        sequences, tokens, heads, head = k.shape
        steps = sequences // 2
        keys, values = (jnp.transpose(x, (0, 2, 3, 1)).reshape(steps, 2 * heads * head, tokens) for x in (k, v))
        half = head // 2
        rounds = sequences // n
        out = pl.pallas_call(
            functools.partial(kernel, n),
            out_shape=jax.ShapeDtypeStruct((sequences, heads // 2, 2 * head), BF16),
            in_specs=[pl.BlockSpec(memory_space=pl.ANY)] * 3,
            out_specs=pl.BlockSpec(memory_space=pltpu.VMEM),
            scratch_shapes=[
                pltpu.VMEM((sequences * heads, head), BF16),
                pltpu.VMEM((SLOTS, 2 * heads * head, tokens), BF16),
                pltpu.VMEM((SLOTS, 2 * heads * head, tokens), BF16),
                pltpu.VMEM((steps, 2, half, 2 * heads), BF16),
                pltpu.VMEM((steps, 2, 2, 2 * heads), F32),
                pltpu.VMEM((rounds, n, half, 2 * heads), BF16),
                pltpu.VMEM((rounds, n, 2, 2 * heads), F32),
                pltpu.VMEM((sequences, heads // 2, 2 * head), BF16),
                pltpu.SemaphoreType.DMA(()),
                pltpu.SemaphoreType.DMA((SLOTS,)),
                pltpu.SemaphoreType.DMA((SLOTS,)),
                pltpu.SemaphoreType.DMA(()),
                pltpu.SemaphoreType.DMA(()),
                pltpu.SemaphoreType.DMA((rounds,)),
                pltpu.SemaphoreType.DMA((rounds,)),
                pltpu.SemaphoreType.DMA(()),
                pltpu.SemaphoreType.DMA((rounds,)),
            ],
            compiler_params=pltpu.CompilerParams(collective_id=0, has_side_effects=True),
        )(q.reshape(sequences * heads, head), keys, values)
        return jnp.concatenate([out[..., :head], out[..., head:]], axis=1)

    return jax.shard_map(
        step,
        mesh=mesh,
        in_specs=(P("dp", None, None), P("dp", "sp", None, None), P("dp", "sp", None, None)),
        out_specs=P("dp", None, None),
        check_vma=False,
    )
```

time: 48.1 us -> 41.2 us (0.86)
  Pallas kernels: 45.6 us -> 38.5 us
  local copies, waits for them, and re-layouts: 2.31 us -> 1.17 us
  other arithmetic: 0 us -> 0.94 us
    pallas_call x1, Pallas kernels: 45.6 us -> 38.5 us  [step(): pl.pallas_call(functools.partial(kernel, n), out_shape=jax.ShapeDtypeStru...]
    reshape x3 -> x0, local copies, waits for them, and re-layouts: 2.31 us -> none  [step(): out.reshape(sequences, half, 2, heads).transpose(0, 3, 2, 1)]
    slice x0 -> x1, local copies, waits for them, and re-layouts: none -> 1.17 us  [step(): return jnp.concatenate([out[..., :head], out[..., head:]], axis=1)]
    concatenate x0 -> x1, other arithmetic: none -> 0.94 us  [step(): return jnp.concatenate([out[..., :head], out[..., head:]], axis=1)]
where the time goes in v2:
time: 41.2 us; the launch traced here: 40.7 us
  Pallas kernels  38.5 us (93%)
  local copies, waits for them, and re-layouts  1.17 us (3%)
  other arithmetic  0.94 us (2%)
    pallas_call x1, Pallas kernels, step(): pl.pallas_call(functools.partial(kernel, n), out_shape=jax.ShapeDtypeStru...  38.5 us
    slice x1, local copies, waits for them, and re-layouts, step(): return jnp.concatenate([out[..., :head], out[..., head:]], axis=1)  1.17 us
    concatenate x1, other arithmetic, step(): return jnp.concatenate([out[..., :head], out[..., head:]], axis=1)  0.94 us

profile of v2, /device:TPU:21, one launch (start us, length us, event | category | flops | bytes accessed | tf_op | source)
XLA Modules:
  0.0 40.7 jit_solution(182684414277116664)
XLA Ops:
  0.0 38.5 %shard_map.37 = bf16[32,32,128]{2,1,0:T(8,128)(2,1)} custom-call(bf16[2048,64]{1,0:T(8,128)(2,1)} %bitcast.9, bf16[16,8192,128]{2,1,0:T(8,128)(2,1)} %bitcast.7, bf16[16,8192,128]{2,1,0:T(8,128)(2,1)} %bitcast.8), custom_call_target="tpu_custom_call" | custom-call | tf_op jit(solution)/shard_map/pallas_call | solution.py:267
  38.5 1.2 %fusion = (bf16[32,32,64]{2,1,0:T(8,128)(2,1)S(1)}, bf16[32,32,64]{2,1,0:T(8,128)(2,1)S(1)}) fusion(bf16[32,32,128]{2,1,0:T(8,128)(2,1)} %shard_map.37), kind=kLoop, calls=%fused_computation.1 | loop fusion | bytes 524288 | tf_op jit(solution)/shard_map/slice | solution.py:293
  39.7 0.9 %pad_maximum_fusion = bf16[32,64,64]{2,1,0:T(8,128)(2,1)} fusion(bf16[32,32,64]{2,1,0:T(8,128)(2,1)S(1)} %get-tuple-element.6, bf16[32,32,64]{2,1,0:T(8,128)(2,1)S(1)} %get-tuple-element.5), kind=kLoop, calls=%fused_computation | loop fusion | flops 524288 | bytes 524288 | tf_op jit(solution)/shard_map/concatenate | solution.py:293

commit v3 on v2

--- a/solution.py
+++ b/solution.py
@@ -102,6 +102,8 @@
     stat_recv,
     done_send,
     done_recv,
+    near_recv,
+    last_sem,
 ):
     me = lax.axis_index("sp")
     cores = 2
@@ -109,6 +111,7 @@
     chip, core = lax.div(me, cores), lax.rem(me, cores)
     steps, rows = k_hbm.shape[0], k_hbm.shape[1]
     rounds = steps // chips
+    last = steps - 1
     heads = q_ref.shape[0] // (steps * cores)
     head = q_ref.shape[1]
 
@@ -126,6 +129,15 @@
     def v_copy(i):
         slot = lax.rem(i, SLOTS)
         return pltpu.make_async_copy(v_hbm.at[block_of(i)], vbuf.at[slot], v_sem.at[slot])
+
+    def rows_of(other):
+        size = rows // cores
+        return pl.ds(pl.multiple_of(lax.rem(core + other, cores) * size, size), size)
+
+    def last_copy(other):
+        return pltpu.make_async_copy(
+            v_hbm.at[block_of(last), rows_of(other)], vbuf.at[last % SLOTS, rows_of(other)], last_sem.at[other]
+        )
 
     def send(i, other):
         r, j = lax.div(i, chips), lax.rem(i, chips)
@@ -177,18 +189,31 @@
         wait_for(parts.at[r, : n - 1], part_recv.at[r])
         seen = functools.reduce(jnp.add, [parts[r, t].astype(F32) * scales[t] for t in range(n)])
         done[r * n + me] = turned(seen / total).astype(BF16)
+        return r * n + me
+
+    def share(which, device, sem):
+        pltpu.make_async_remote_copy(
+            done.at[which], done.at[which], done_send, sem, device_id={"sp": device}, device_id_type=MESH
+        ).start()
+
+    def gather(r):
         for j in range(chips):
             for other in (1, 0):
-                if j == chips - 1 and other == 0:
-                    continue
-                pltpu.make_async_remote_copy(
-                    done.at[r * n + me],
-                    done.at[r * n + me],
-                    done_send,
-                    done_recv.at[r],
-                    device_id={"sp": chip_of(j) * cores + lax.rem(core + other, cores)},
-                    device_id_type=MESH,
-                ).start()
+                if j < chips - 1 or other:
+                    share(r * n + me, chip_of(j) * cores + lax.rem(core + other, cores), done_recv.at[r])
+
+    def relay(r):
+        partner = chip * cores + lax.rem(core + 1, cores)
+        for j in range(chips - 1):
+            share(r * n + me, chip_of(j) * cores + core, near_recv.at[j])
+            if j == 0:
+                share(r * n + me, chip_of(j) * cores + lax.rem(core + 1, cores), done_recv.at[r])
+        share(r * n + me, partner, done_recv.at[r])
+        for j in reversed(range(chips - 1)):
+            wait_for(done.at[0], near_recv.at[j])
+            if j > 0:
+                away = (chips // 2 - (j + 1) // 2) * (2 * (j % 2) - 1)
+                share(r * n + lax.rem(chip - away + chips, chips) * cores + core, partner, done_recv.at[r])
 
     q_copy = pltpu.make_async_copy(q_hbm, q_ref, q_sem)
     q_copy.start()
@@ -213,9 +238,14 @@
         def _():
             k_copy(i + SLOTS).start()
 
-        @pl.when(i + SLOTS - 1 < steps)
+        @pl.when(i + SLOTS - 1 < last)
         def _():
             v_copy(i + SLOTS - 1).start()
+
+        @pl.when(i + SLOTS - 1 == last)
+        def _():
+            for other in (1, 0):
+                last_copy(other).start()
 
         @pl.when(i > 0)
         def _():
@@ -236,23 +266,34 @@
         until = (r + 1) * chips + EARLY
         weights = lax.fori_loop(first, until, step, weights)
         finish(r)
+        gather(r)
         first = until
-    weights = lax.fori_loop(first, steps - 1, step, weights)
-    last = steps - 1
-    v_copy(last).wait()
-    send(last - 1, 1)
-    send(last - 1, 0)
-    for j in range(cores):
-        see(last, j, weights[j])
-    send(last, 1)
+    weights = lax.fori_loop(first, last, step, weights)
+    for other in (1, 0):
+        send(last - 1, other)
+    mine = [x.astype(F32) for x in weights]
+    for other in (1, 0):
+        ours = jnp.where(lax.rem(core + other, cores) == 0, *mine).astype(BF16)
+        last_copy(other).wait()
+        part[last, lax.rem(core + other, cores)] = seen_of(ours, vbuf.at[last % SLOTS, rows_of(other)], head).astype(BF16)
+        if other:
+            send(last, other)
     finish(rounds - 1)
+    relay(rounds - 1)
     wait_for(parts.at[:, : n - 1], part_send)
     wait_for(stats.at[:, : n - 1], stat_send)
     for r in range(rounds):
         wait_for(done.at[: n - 1], done_send)
-    for r in range(rounds):
+    for r in range(rounds - 1):
         wait_for(done.at[: n - 1], done_recv.at[r])
+    wait_for(done.at[:chips], done_recv.at[rounds - 1])
     out_ref[...] = done[...]
+
+
+def unpack(packed_ref, out_ref):
+    half, head = packed_ref.shape[1], out_ref.shape[2]
+    out_ref[:, :half] = packed_ref[:, :, :head]
+    out_ref[:, half:] = packed_ref[:, :, head:]
 
 
 def solution(mesh):
@@ -266,7 +307,7 @@
         rounds = sequences // n
         out = pl.pallas_call(
             functools.partial(kernel, n),
-            out_shape=jax.ShapeDtypeStruct((sequences, heads // 2, 2 * head), BF16),
+            out_shape=pltpu.VMEM((sequences, heads // 2, 2 * head), BF16),
             in_specs=[pl.BlockSpec(memory_space=pl.ANY)] * 3,
             out_specs=pl.BlockSpec(memory_space=pltpu.VMEM),
             scratch_shapes=[
@@ -287,10 +328,17 @@
                 pltpu.SemaphoreType.DMA((rounds,)),
                 pltpu.SemaphoreType.DMA(()),
                 pltpu.SemaphoreType.DMA((rounds,)),
+                pltpu.SemaphoreType.DMA((n // 2 - 1,)),
+                pltpu.SemaphoreType.DMA((2,)),
             ],
             compiler_params=pltpu.CompilerParams(collective_id=0, has_side_effects=True),
         )(q.reshape(sequences * heads, head), keys, values)
-        return jnp.concatenate([out[..., :head], out[..., head:]], axis=1)
+        return pl.pallas_call(
+            unpack,
+            out_shape=jax.ShapeDtypeStruct(q.shape, BF16),
+            in_specs=[pl.BlockSpec(memory_space=pltpu.VMEM)],
+            out_specs=pl.BlockSpec(memory_space=pltpu.VMEM),
+        )(pltpu.with_memory_space_constraint(out, pltpu.VMEM))
 
     return jax.shard_map(
         step,

time: 41.2 us -> 40.2 us (0.976); the launches traced: 40.7 us -> 40.1 us
  Pallas kernels: 38.5 us -> 40.1 us
  local copies, waits for them, and re-layouts: 1.17 us -> 0 us
  other arithmetic: 0.94 us -> 0 us
    pallas_call x1 -> x2, Pallas kernels: 38.5 us -> 40.1 us  [the longest x1 39.1 us: step(): pl.pallas_call(functools.partial(kernel, n), out_shape=pltpu.VMEM((sequen...]
    slice x1 -> x0, local copies, waits for them, and re-layouts: 1.17 us -> none  [step(): return jnp.concatenate([out[..., :head], out[..., head:]], axis=1)]
    concatenate x1 -> x0, other arithmetic: 0.94 us -> none  [step(): return jnp.concatenate([out[..., :head], out[..., head:]], axis=1)]
where the time goes in v3:
time: 40.2 us; the launch traced here: 40.1 us
  Pallas kernels  40.1 us (100%)
    pallas_call x1, Pallas kernels, step(): pl.pallas_call(functools.partial(kernel, n), out_shape=pltpu.VMEM((sequen...  39.1 us
    pallas_call x1, Pallas kernels, step(): pl.pallas_call(unpack, out_shape=jax.ShapeDtypeStruct(q.shape, BF16), in_...  1.01 us

profile of v3, /device:TPU:21, one launch (start us, length us, event | category | flops | bytes accessed | tf_op | source)
XLA Modules:
  0.0 40.1 jit_solution(17634587682590256216)
XLA Ops:
  0.0 39.1 %shard_map.37.packed_ref = bf16[32,32,128]{2,1,0:T(8,128)(2,1)S(1)} custom-call(bf16[2048,64]{1,0:T(8,128)(2,1)} %bitcast.9, bf16[16,8192,128]{2,1,0:T(8,128)(2,1)} %bitcast.7, bf16[16,8192,128]{2,1,0:T(8,128)(2,1)} %bitcast.8), custom_call_target="tpu_custom_call" | custom-call | tf_op jit(solution)/shard_map/pallas_call | solution.py:308
  39.1 1.0 %shard_map.38 = bf16[32,64,64]{2,1,0:T(8,128)(2,1)} custom-call(bf16[32,32,128]{2,1,0:T(8,128)(2,1)S(1)} %shard_map.37.packed_ref), custom_call_target="tpu_custom_call" | custom-call | tf_op jit(solution)/shard_map/pallas_call | solution.py:336

commit v4 on v3

--- a/solution.py
+++ b/solution.py
@@ -10,6 +10,7 @@
 MESH = pl.DeviceIdType.MESH
 F32, BF16 = jnp.float32, jnp.bfloat16
 SLOTS = 4
+QUIET = 4
 EARLY = 3
 ROWS = 16
 
@@ -228,9 +229,8 @@
     q_copy.wait()
     k_copy(0).wait()
     weights = tuple(score(0, j) for j in range(cores))
-    pl.semaphore_wait(barrier, n - 1)
-
-    def step(i, weights):
+
+    def step(first, i, weights):
         k_copy(i + 1).wait()
         v_copy(i).wait()
 
@@ -247,13 +247,12 @@
             for other in (1, 0):
                 last_copy(other).start()
 
-        @pl.when(i > 0)
-        def _():
-            send(i - 1, 1)
-
-        @pl.when(lax.rem(i, chips) > 0)
-        def _():
-            send(i - 1, 0)
+        if first:
+
+            @pl.when(i > first)
+            def _():
+                for other in (1, 0):
+                    send(i - 1, other)
 
         later = []
         for j in range(cores):
@@ -261,14 +260,25 @@
             see(i, j, weights[j])
         return tuple(later)
 
-    first = 0
+    weights = lax.fori_loop(0, QUIET, functools.partial(step, None), weights)
+    pl.semaphore_wait(barrier, n - 1)
+
+    def send_both(i, _):
+        for other in (1, 0):
+            send(i, other)
+
+    lax.fori_loop(0, QUIET, send_both, None)
+    first = QUIET
     for r in range(rounds - 1):
-        until = (r + 1) * chips + EARLY
-        weights = lax.fori_loop(first, until, step, weights)
+        middle, until = (r + 1) * chips, (r + 1) * chips + EARLY
+        weights = lax.fori_loop(first, middle, functools.partial(step, first), weights)
+        send(middle - 1, 1)
+        weights = lax.fori_loop(middle, until, functools.partial(step, middle), weights)
+        send_both(until - 1, None)
         finish(r)
         gather(r)
         first = until
-    weights = lax.fori_loop(first, last, step, weights)
+    weights = lax.fori_loop(first, last, functools.partial(step, first), weights)
     for other in (1, 0):
         send(last - 1, other)
     mine = [x.astype(F32) for x in weights]

time: 40.2 us -> 39.5 us (0.983)
  Pallas kernels: 40.1 us -> 39.4 us
    pallas_call x1, Pallas kernels: 39.1 us -> 38.4 us  [step(): pl.pallas_call(functools.partial(kernel, n), out_shape=pltpu.VMEM((sequen...]
where the time goes in v4:
time: 39.5 us; the launch traced here: 39.4 us
  Pallas kernels  39.4 us (100%)
    pallas_call x1, Pallas kernels, step(): pl.pallas_call(functools.partial(kernel, n), out_shape=pltpu.VMEM((sequen...  38.4 us
    pallas_call x1, Pallas kernels, step(): pl.pallas_call(unpack, out_shape=jax.ShapeDtypeStruct(q.shape, BF16), in_...  1.01 us

profile of v4, /device:TPU:21, one launch (start us, length us, event | category | flops | bytes accessed | tf_op | source)
XLA Modules:
  0.0 39.4 jit_solution(10258138546261382352)
XLA Ops:
  0.0 38.4 %shard_map.37.packed_ref = bf16[32,32,128]{2,1,0:T(8,128)(2,1)S(1)} custom-call(bf16[2048,64]{1,0:T(8,128)(2,1)} %bitcast.9, bf16[16,8192,128]{2,1,0:T(8,128)(2,1)} %bitcast.7, bf16[16,8192,128]{2,1,0:T(8,128)(2,1)} %bitcast.8), custom_call_target="tpu_custom_call" | custom-call | tf_op jit(solution)/shard_map/pallas_call | solution.py:318
  38.4 1.0 %shard_map.38 = bf16[32,64,64]{2,1,0:T(8,128)(2,1)} custom-call(bf16[32,32,128]{2,1,0:T(8,128)(2,1)S(1)} %shard_map.37.packed_ref), custom_call_target="tpu_custom_call" | custom-call | tf_op jit(solution)/shard_map/pallas_call | solution.py:346

commit v5 on v4

--- a/solution.py
+++ b/solution.py
@@ -123,13 +123,18 @@
     def block_of(i):
         return lax.div(i, chips) * chips + chip_of(lax.rem(i, chips))
 
-    def k_copy(i):
+    def k_copy(i, block=0):
         slot = lax.rem(i, SLOTS)
-        return pltpu.make_async_copy(k_hbm.at[block_of(i)], kbuf.at[slot], k_sem.at[slot])
-
-    def v_copy(i):
+        return pltpu.make_async_copy(k_hbm.at[block], kbuf.at[slot], k_sem.at[slot])
+
+    def v_copy(i, block=0):
         slot = lax.rem(i, SLOTS)
-        return pltpu.make_async_copy(v_hbm.at[block_of(i)], vbuf.at[slot], v_sem.at[slot])
+        return pltpu.make_async_copy(v_hbm.at[block], vbuf.at[slot], v_sem.at[slot])
+
+    def first_copy(j):
+        size = rows // cores
+        own = pl.ds(j * size, size)
+        return pltpu.make_async_copy(k_hbm.at[block_of(0), own], kbuf.at[0, own], last_sem.at[j])
 
     def rows_of(other):
         size = rows // cores
@@ -140,11 +145,11 @@
             v_hbm.at[block_of(last), rows_of(other)], vbuf.at[last % SLOTS, rows_of(other)], last_sem.at[other]
         )
 
-    def send(i, other):
-        r, j = lax.div(i, chips), lax.rem(i, chips)
+    def send(i, other, r, owner):
+        j = i - r * chips
         to = lax.rem(core + other, cores)
         slot = j * cores + 1 - other
-        device = {"sp": chip_of(j) * cores + to}
+        device = {"sp": owner * cores + to}
         pltpu.make_async_remote_copy(
             part.at[i, to],
             parts.at[r, slot],
@@ -162,8 +167,8 @@
             device_id_type=MESH,
         ).start()
 
-    def score(i, j):
-        q = q_ref[pl.ds(pl.multiple_of((block_of(i) * cores + j) * heads, heads), heads), :]
+    def score(i, j, block):
+        q = q_ref[pl.ds(pl.multiple_of((block * cores + j) * heads, heads), heads), :]
         size = rows // cores
         keys = kbuf.at[lax.rem(i, SLOTS), j * size : (j + 1) * size]
         weights, total, high = weights_of(scores_of(q, keys, head))
@@ -219,28 +224,36 @@
     q_copy = pltpu.make_async_copy(q_hbm, q_ref, q_sem)
     q_copy.start()
     for i in range(SLOTS):
-        k_copy(i).start()
+        if i:
+            k_copy(i, block_of(i)).start()
+        else:
+            for j in range(cores):
+                first_copy(j).start()
         if i < SLOTS - 1:
-            v_copy(i).start()
+            v_copy(i, block_of(i)).start()
     barrier = pltpu.get_barrier_semaphore()
     for away in range(1, n):
         pl.semaphore_signal(barrier, inc=1, device_id={"sp": lax.rem(me + away, n)}, device_id_type=MESH)
 
     q_copy.wait()
-    k_copy(0).wait()
-    weights = tuple(score(0, j) for j in range(cores))
-
-    def step(first, i, weights):
+    start = block_of(0)
+    weights = []
+    for j in range(cores):
+        first_copy(j).wait()
+        weights.append(score(0, j, start))
+
+    def step(first, i, state):
+        blocks, weights = state
         k_copy(i + 1).wait()
         v_copy(i).wait()
 
         @pl.when(i + SLOTS < steps)
         def _():
-            k_copy(i + SLOTS).start()
+            k_copy(i + SLOTS, blocks[-1]).start()
 
         @pl.when(i + SLOTS - 1 < last)
         def _():
-            v_copy(i + SLOTS - 1).start()
+            v_copy(i + SLOTS - 1, blocks[-2]).start()
 
         @pl.when(i + SLOTS - 1 == last)
         def _():
@@ -251,43 +264,46 @@
 
             @pl.when(i > first)
             def _():
+                r = first // chips
                 for other in (1, 0):
-                    send(i - 1, other)
+                    send(i - 1, other, r, blocks[0] - r * chips)
 
         later = []
         for j in range(cores):
-            later.append(score(i + 1, j))
+            later.append(score(i + 1, j, blocks[2]))
             see(i, j, weights[j])
-        return tuple(later)
-
-    weights = lax.fori_loop(0, QUIET, functools.partial(step, None), weights)
+        return (*blocks[1:], block_of(lax.rem(i + SLOTS + 1, steps))), tuple(later)
+
+    state = (start, *(block_of(i) for i in range(SLOTS + 1))), tuple(weights)
+    state = lax.fori_loop(0, QUIET, functools.partial(step, None), state)
     pl.semaphore_wait(barrier, n - 1)
 
     def send_both(i, _):
         for other in (1, 0):
-            send(i, other)
+            send(i, other, 0, chip_of(i))
 
     lax.fori_loop(0, QUIET, send_both, None)
     first = QUIET
     for r in range(rounds - 1):
         middle, until = (r + 1) * chips, (r + 1) * chips + EARLY
-        weights = lax.fori_loop(first, middle, functools.partial(step, first), weights)
-        send(middle - 1, 1)
-        weights = lax.fori_loop(middle, until, functools.partial(step, middle), weights)
-        send_both(until - 1, None)
+        state = lax.fori_loop(first, middle, functools.partial(step, first), state)
+        send(middle - 1, 1, r, chip)
+        state = lax.fori_loop(middle, until, functools.partial(step, middle), state)
+        for other in (1, 0):
+            send(until - 1, other, r + 1, chip_of(EARLY - 1))
         finish(r)
         gather(r)
         first = until
-    weights = lax.fori_loop(first, last, functools.partial(step, first), weights)
+    _, weights = lax.fori_loop(first, last, functools.partial(step, first), state)
     for other in (1, 0):
-        send(last - 1, other)
+        send(last - 1, other, rounds - 1, chip_of(chips - 2))
     mine = [x.astype(F32) for x in weights]
     for other in (1, 0):
         ours = jnp.where(lax.rem(core + other, cores) == 0, *mine).astype(BF16)
         last_copy(other).wait()
         part[last, lax.rem(core + other, cores)] = seen_of(ours, vbuf.at[last % SLOTS, rows_of(other)], head).astype(BF16)
         if other:
-            send(last, other)
+            send(last, other, rounds - 1, chip)
     finish(rounds - 1)
     relay(rounds - 1)
     wait_for(parts.at[:, : n - 1], part_send)

time: 39.5 us -> 39.4 us (level)
  no operation moved by 1% of the time
where the time goes in v5:
time: 39.4 us; the launch traced here: 39.3 us
  Pallas kernels  39.3 us (100%)
    pallas_call x1, Pallas kernels, step(): pl.pallas_call(functools.partial(kernel, n), out_shape=pltpu.VMEM((sequen...  38.3 us
    pallas_call x1, Pallas kernels, step(): pl.pallas_call(unpack, out_shape=jax.ShapeDtypeStruct(q.shape, BF16), in_...  1.01 us

profile of v5, /device:TPU:21, one launch (start us, length us, event | category | flops | bytes accessed | tf_op | source)
XLA Modules:
  0.0 39.3 jit_solution(8365069810959891885)
XLA Ops:
  0.0 38.3 %shard_map.37.packed_ref = bf16[32,32,128]{2,1,0:T(8,128)(2,1)S(1)} custom-call(bf16[2048,64]{1,0:T(8,128)(2,1)} %bitcast.9, bf16[16,8192,128]{2,1,0:T(8,128)(2,1)} %bitcast.7, bf16[16,8192,128]{2,1,0:T(8,128)(2,1)} %bitcast.8), custom_call_target="tpu_custom_call" | custom-call | tf_op jit(solution)/shard_map/pallas_call | solution.py:334
  38.3 1.0 %shard_map.38 = bf16[32,64,64]{2,1,0:T(8,128)(2,1)} custom-call(bf16[32,32,128]{2,1,0:T(8,128)(2,1)S(1)} %shard_map.37.packed_ref), custom_call_target="tpu_custom_call" | custom-call | tf_op jit(solution)/shard_map/pallas_call | solution.py:362

commit v6 on v5

--- a/solution.py
+++ b/solution.py
@@ -9,7 +9,7 @@
 
 MESH = pl.DeviceIdType.MESH
 F32, BF16 = jnp.float32, jnp.bfloat16
-SLOTS = 4
+SLOTS = 3
 QUIET = 4
 EARLY = 3
 ROWS = 16
@@ -247,19 +247,6 @@
         k_copy(i + 1).wait()
         v_copy(i).wait()
 
-        @pl.when(i + SLOTS < steps)
-        def _():
-            k_copy(i + SLOTS, blocks[-1]).start()
-
-        @pl.when(i + SLOTS - 1 < last)
-        def _():
-            v_copy(i + SLOTS - 1, blocks[-2]).start()
-
-        @pl.when(i + SLOTS - 1 == last)
-        def _():
-            for other in (1, 0):
-                last_copy(other).start()
-
         if first:
 
             @pl.when(i > first)
@@ -267,6 +254,19 @@
                 r = first // chips
                 for other in (1, 0):
                     send(i - 1, other, r, blocks[0] - r * chips)
+
+        @pl.when(i + SLOTS < steps)
+        def _():
+            k_copy(i + SLOTS, blocks[-1]).start()
+
+        @pl.when(i + SLOTS - 1 < last)
+        def _():
+            v_copy(i + SLOTS - 1, blocks[-2]).start()
+
+        @pl.when(i + SLOTS - 1 == last)
+        def _():
+            for other in (1, 0):
+                last_copy(other).start()
 
         later = []
         for j in range(cores):

time: 39.4 us -> 39 us (0.990)
  no operation moved by 1% of the time
where the time goes in v6:
time: 39 us
  Pallas kernels  39 us (100%)
    pallas_call x1, Pallas kernels, step(): pl.pallas_call(functools.partial(kernel, n), out_shape=pltpu.VMEM((sequen...  37.9 us
    pallas_call x1, Pallas kernels, step(): pl.pallas_call(unpack, out_shape=jax.ShapeDtypeStruct(q.shape, BF16), in_...  1.01 us

profile of v6, /device:TPU:21, one launch (start us, length us, event | category | flops | bytes accessed | tf_op | source)
XLA Modules:
  0.0 39.0 jit_solution(16001452951598776317)
XLA Ops:
  0.0 37.9 %shard_map.37.packed_ref = bf16[32,32,128]{2,1,0:T(8,128)(2,1)S(1)} custom-call(bf16[2048,64]{1,0:T(8,128)(2,1)} %bitcast.9, bf16[16,8192,128]{2,1,0:T(8,128)(2,1)} %bitcast.7, bf16[16,8192,128]{2,1,0:T(8,128)(2,1)} %bitcast.8), custom_call_target="tpu_custom_call" | custom-call | tf_op jit(solution)/shard_map/pallas_call | solution.py:334
  38.0 1.0 %shard_map.38 = bf16[32,64,64]{2,1,0:T(8,128)(2,1)} custom-call(bf16[32,32,128]{2,1,0:T(8,128)(2,1)S(1)} %shard_map.37.packed_ref), custom_call_target="tpu_custom_call" | custom-call | tf_op jit(solution)/shard_map/pallas_call | solution.py:362

commit v7 on v6

--- a/solution.py
+++ b/solution.py
@@ -244,8 +244,6 @@
 
     def step(first, i, state):
         blocks, weights = state
-        k_copy(i + 1).wait()
-        v_copy(i).wait()
 
         if first:
 
@@ -254,6 +252,9 @@
                 r = first // chips
                 for other in (1, 0):
                     send(i - 1, other, r, blocks[0] - r * chips)
+
+        k_copy(i + 1).wait()
+        v_copy(i).wait()
 
         @pl.when(i + SLOTS < steps)
         def _():

time: 39 us -> 38.9 us (level)
  no operation moved by 1% of the time
where the time goes in v7:
time: 38.9 us; the launch traced here: 38.8 us
  Pallas kernels  38.8 us (100%)
    pallas_call x1, Pallas kernels, step(): pl.pallas_call(functools.partial(kernel, n), out_shape=pltpu.VMEM((sequen...  37.8 us
    pallas_call x1, Pallas kernels, step(): pl.pallas_call(unpack, out_shape=jax.ShapeDtypeStruct(q.shape, BF16), in_...  1.01 us

profile of v7, /device:TPU:21, one launch (start us, length us, event | category | flops | bytes accessed | tf_op | source)
XLA Modules:
  0.0 38.8 jit_solution(9552814982453014099)
XLA Ops:
  0.0 37.8 %shard_map.37.packed_ref = bf16[32,32,128]{2,1,0:T(8,128)(2,1)S(1)} custom-call(bf16[2048,64]{1,0:T(8,128)(2,1)} %bitcast.9, bf16[16,8192,128]{2,1,0:T(8,128)(2,1)} %bitcast.7, bf16[16,8192,128]{2,1,0:T(8,128)(2,1)} %bitcast.8), custom_call_target="tpu_custom_call" | custom-call | tf_op jit(solution)/shard_map/pallas_call | solution.py:335
  37.8 1.0 %shard_map.38 = bf16[32,64,64]{2,1,0:T(8,128)(2,1)} custom-call(bf16[32,32,128]{2,1,0:T(8,128)(2,1)S(1)} %shard_map.37.packed_ref), custom_call_target="tpu_custom_call" | custom-call | tf_op jit(solution)/shard_map/pallas_call | solution.py:363
